TPU v7x, 32 devices: a whole 2x2x4 slice. The times are simulated.
32 devices in a mesh: parts: 2 (over y), section: 2 (over core), tp: 8 (over z, x).
Axes of the slice: x: 2, y: 2, z: 4, core: 2. Of those that a mesh axis runs over, the one named last changes fastest.
Arguments:
- prompt_rows: bfloat16 [128, 8192], P(('parts', 'section', 'tp')), parts along dimension 0, may hold values from -72 to 72
- query_weight: bfloat16 [8192, 8192], P(None, 'tp'), may hold values from -0.0625 to 0.0625
- cache_weight: bfloat16 [8, 8192, 256], P('tp'), may hold values from -1 to 1, as said below
- output_weight: bfloat16 [8192, 8192], P('tp'), may hold values from -0.0625 to 0.0625
- documents: int32 [128], P('parts'), parts along dimension 0, may hold values from 0 to 3, never falling along the last dimension, each value on 1 to 32 neighbouring positions
- page_table: int32 [24], P('parts'), parts along dimension 0, may hold values from 0 to 15, as said below
Outputs:
- branch_output: bfloat16 [128, 8192], P(('parts', 'section', 'tp')), parts along dimension 0
- page_pool: bfloat16 [32, 8, 2048], P(('parts', 'section', 'tp')), parts along dimension 0
There are 2 independent parts, one for each index of `parts`. A program takes and returns all parts, laid end to end along the dimension named above; an argument that names none is the same for every part. Nothing has to cross between parts.
Inputs may be any that keep to these rules, and one draw needn't show every extreme that they name: `cache_weight`: entry t equals entry u whenever t == u. `documents`: ids never fall along the tokens; there are 4 prompts of 1 to 32 tokens, one of exactly 32. `page_table`: entries are distinct pool slots; slot q is owned by the device of index q along section+tp (one slot per device). Entries beyond the number of pages are not used.
All inputs are finite; a program needn't handle non-finite values.
Results may differ from a plain program's by a relative error of at most 0.0085.
The roundings to bfloat16 on the way count: a program that leaves them out, or rounds other values in their place, can miss the bound.
Values may be sent and summed in bfloat16 or wider, within the bound.
No kernel may reach another device: no remote copies, remote signals or barrier semaphores. Data moves between devices by JAX's collectives and lax.ppermute only.
A program may use at most 64 MiB of HBM per device.

v0:
```python
import jax
import jax.numpy as jnp
from jax import lax
from jax.sharding import PartitionSpec as P

KV_HEADS = 8
HEAD = 128
PAGE = 8
rope_base = 500000.0


def from_partner(value, axis, distance):
    mask = 2**distance
    pairs = [(source, source ^ mask) for source in range(lax.axis_size(axis))]
    return lax.ppermute(value, axis, pairs)


def document_layout(documents):
    count = documents.shape[0]
    places = jnp.arange(count, dtype=jnp.int32)
    begins = jnp.concatenate([jnp.ones((1,), dtype=bool), documents[1:] != documents[:-1]])
    firsts = lax.cummax(jnp.where(begins, places, jnp.zeros_like(places)), axis=0)
    offsets = places - firsts
    starts = (offsets % PAGE == 0).astype(jnp.int32)
    pages = jnp.cumsum(starts) - 1
    return (offsets, pages)


def rope_tables(offsets, width):
    half_width = width // 2
    freqs = rope_base ** (-(jnp.arange(half_width, dtype=jnp.float32) * 2.0 / width))
    angles = offsets.astype(jnp.float32)[:, None] * freqs[None, :]
    return (jnp.cos(angles), jnp.sin(angles))


def rotate(values, cosines, sines):
    half_width = values.shape[-1] // 2
    first = values[..., :half_width]
    second = values[..., half_width:]
    return jnp.concatenate(
        [first * cosines - second * sines, second * cosines + first * sines], axis=-1
    )


def finish_cache(keyvals, cosines, sines):
    rotated = rotate(keyvals[:, :HEAD], cosines, sines)
    return jnp.concatenate([rotated, keyvals[:, HEAD:]], axis=1).astype(jnp.bfloat16)


def body(prompt_rows, query_weight, cache_weight, output_weight, documents, page_table):
    tp_count = lax.axis_size("tp")
    owners = lax.axis_size(("section", "tp"))
    section = lax.axis_index("section")
    column = lax.axis_index("tp")
    rows_dev = prompt_rows.shape[0]
    half_rows = rows_dev * tp_count
    total_rows = 2 * half_rows
    query_width = query_weight.shape[1]
    query_heads = query_width // HEAD
    replicas = tp_count // KV_HEADS
    slice_width = HEAD // replicas
    head_weight = cache_weight[0]
    offsets, pages = document_layout(documents)
    cosines, sines = rope_tables(offsets, HEAD)
    own_start = section * half_rows
    own_cos = lax.dynamic_slice_in_dim(cosines, own_start, half_rows, 0)
    own_sin = lax.dynamic_slice_in_dim(sines, own_start, half_rows, 0)
    piece = lax.all_gather(prompt_rows, "tp", axis=0, tiled=True)
    query_rows = jnp.dot(piece, query_weight, preferred_element_type=jnp.float32)
    cache_rows = jnp.dot(piece, head_weight, preferred_element_type=jnp.float32)
    joined = jnp.concatenate([query_rows, cache_rows], axis=1)
    query_part = joined[:, :query_width]
    cache_half = finish_cache(joined[:, query_width:], own_cos, own_sin)
    other = from_partner(cache_half, "section", 0)
    lower = jnp.where(section == 0, cache_half, other)
    upper = jnp.where(section == 0, other, cache_half)
    cache_all = jnp.concatenate([lower, upper], axis=0)
    queries = query_part.reshape(half_rows, query_heads, HEAD)
    queries = rotate(queries, own_cos[:, None, :], own_sin[:, None, :]).astype(jnp.bfloat16)
    keys = cache_all[:, :HEAD]
    values = cache_all[:, HEAD:]
    places = jnp.arange(total_rows, dtype=jnp.int32)
    query_places = own_start + jnp.arange(half_rows, dtype=jnp.int32)
    query_docs = lax.dynamic_slice_in_dim(documents, own_start, half_rows, 0)
    allowed = (query_docs[:, None] == documents[None, :]) & (
        places[None, :] <= query_places[:, None]
    )
    scale = 1.0 / HEAD**0.5
    scores = jnp.einsum("qhd,kd->hqk", queries, keys, preferred_element_type=jnp.float32) * scale
    scores = jnp.where(allowed[None, :, :], scores, -jnp.inf)
    weights = jax.nn.softmax(scores, axis=-1).astype(jnp.bfloat16)
    mixed = jnp.einsum("hqk,kd->qhd", weights, values, preferred_element_type=jnp.float32)
    attention = mixed.astype(jnp.bfloat16).reshape(half_rows, query_heads * HEAD)
    summed = lax.psum_scatter(
        jnp.dot(attention, output_weight, preferred_element_type=jnp.float32),
        "tp",
        scatter_dimension=0,
        tiled=True,
    )
    branch_output = summed.astype(jnp.bfloat16)
    column_start = section * HEAD + column % replicas * slice_width
    share = lax.dynamic_slice_in_dim(cache_all, column_start, slice_width, 1)
    capacity = rows_dev // 4 * PAGE
    row_of = page_table[pages] * PAGE + offsets % PAGE
    outgoing = jnp.zeros((owners * capacity, slice_width), jnp.bfloat16).at[row_of].set(share)
    outgoing = outgoing.reshape(owners, capacity, slice_width)
    arrived = lax.all_to_all(outgoing, ("section", "tp"), split_axis=0, concat_axis=2, tiled=True)
    return (branch_output, arrived)


def solution(mesh):
    return jax.shard_map(
        body,
        mesh=mesh,
        in_specs=(
            P(("parts", "section", "tp"), None),
            P(None, "tp"),
            P("tp", None, None),
            P("tp", None),
            P("parts"),
            P("parts"),
        ),
        out_specs=(P(("parts", "section", "tp"), None), P(("parts", "section", "tp"), None, None)),
        check_vma=False,
    )
```

profile of v0, /device:TPU:0, one launch (start us, length us, event | category | flops | bytes accessed | tf_op | source)
XLA Modules:
  0.0 150.3 jit_solution(4755525236660970167)
XLA Ops:
  0.7 1.8 %fusion.44 = (s32[1]{0:T(128)}, s32[1]{0:T(128)}, s32[1]{0:T(128)}, s32[1]{0:T(128)}, s32[1]{0:T(128)}, /*index=5*/s32[1]{0:T(128)}, s32[1]{0:T(128)}, s32[1]{0:...) fusion(s32[12]{0:T(128)} %param.11), kind=kLoop, calls=%fused_computation.74 | loop fusion | bytes 96 | tf_op jit(solution)/shard_map/gather | solution.py:104
  2.5 0.8 compare_bitcast_fusion
  3.3 0.1 copy.18
  3.4 0.1 reduce-window.6
  3.6 0.1 reduce-window.9
  3.7 0.2 compare_reduce_fusion.4
  3.9 4.4 %select_reduce_fusion = s32[64]{0:T(128)S(1)} fusion(s32[]{:T(128)} %bitcast.12, s32[]{:T(128)} %bitcast.13, s32[]{:T(128)} %bitcast.14, s32[]{:T(128)} %bitcast.15, s32[]{:T(128)} %bitcast.16, s32[]{:T(128)} %bitcast.18, s32[]{:T(128)} %bitcast.17, s32[64,1]{1,0:T(8,128)S(1)} %reduce-window.9), kind=kLoop, calls=%fused_computation.35 | loop fusion | flops 1024 | bytes 540 | tf_op jit(solution)/shard_map/gather | solution.py:104
  8.3 3.2 %fusion.31 = s32[64,1]{0,1:T(1,128)S(1)} fusion(pred[64]{0:T(512)(128)(4,1)S(1)} %get-tuple-element.8, pred[64]{0:T(512)(128)(4,1)S(1)} %get-tuple-element.5, pred[64]{0:T(512)(128)(4,1)S(1)} %get-tuple-element.6, pred[64]{0:T(512)(128)(4,1)S(1)} %get-tuple-element.7, pred[64]{0:T(512)(128)(4,1)S(1)} %get-tuple-element.4, s32[64]{0:T(128)S(1)} %select_reduce_fusion, ...), kind=kLoop, calls=%fused_computation.63 | loop fusion | flops 384 | bytes 852 | tf_op jit(solution)/shard_map/mul | solution.py:104
  11.5 0.1 copy.22
  11.6 0.1 fusion.15
  11.7 33.3 %all-gather = bf16[8,4,8192]{2,1,0:T(4,128)(2,1)S(1)} all-gather(bf16[1,4,8192]{2,1,0:T(4,128)(2,1)} %bitcast.64), channel_id=1, replica_groups=mesh['parts'=2,'section'=2,'tp'=8] {'tp'}, dimensions={0}, use_global_device_ids=true | all-gather | bytes 589824 | tf_op jit(solution)/shard_map/all_gather | solution.py:68
  45.0 0.1 reshape.264
  45.1 3.0 %fusion.1 = f32[32,256]{1,0:T(8,128)S(1)} fusion(bf16[32,8192]{1,0:T(8,128)(2,1)S(1)} %reshape.264, bf16[1,8192,256]{2,1,0:T(8,128)(2,1)} %param.8), kind=kOutput, calls=%fused_computation.2 | convolution fusion | flops 134217728 | bytes 4751360 | tf_op jit(solution)/shard_map/dot_general | solution.py:70
  48.5 0.7 dynamic_slice.14
  49.2 8.7 %convolution_bitcast_fusion = f32[4,8,8,128]{3,1,2,0:T(8,128)S(1)} fusion(bf16[32,8192]{1,0:T(8,128)(2,1)S(1)} %reshape.264, bf16[8192,1024]{1,0:T(8,128)(2,1)} %param.7), kind=kOutput, calls=%fused_computation.6 | convolution fusion | flops 536870912 | bytes 17432576 | tf_op jit(solution)/shard_map/dot_general | solution.py:69
  58.3 0.6 dynamic-slice
  59.6 1.3 scatter_custom_fusion
  60.9 5.8 %all-to-all-start = ((bf16[16,8,128]{2,1,0:T(8,128)(2,1)}), bf16[16,8,128]{2,1,0:T(8,128)(2,1)S(1)}, u32[]{:S(2)}, u32[]{:S(2)}) async-start(bf16[16,8,128]{2,1,0:T(8,128)(2,1)} %bitcast.20), calls=%async_computation | async-start | bytes 65536 | tf_op jit(solution)/shard_map/all_to_all | solution.py:107
  66.7 0.4 fusion.45
  67.2 0.2 fusion.7
  67.4 8.7 %fusion.8 = f32[32,8192]{1,0:T(8,128)S(1)} fusion(bf16[1024,8192]{1,0:T(8,128)(2,1)} %param.9, bf16[8,4,8,128]{3,2,1,0:T(8,128)(2,1)S(1)} %fusion.7), kind=kOutput, calls=%fused_computation.18 | convolution fusion | flops 536870912 | bytes 17891328 | tf_op jit(solution)/shard_map/dot_general | solution.py:95
  76.1 72.9 %all-reduce.2 = bf16[32,8192]{1,0:T(8,128)(2,1)S(1)} all-reduce(f32[32,8192]{1,0:T(8,128)S(1)} %fusion.8), channel_id=2, replica_groups=mesh['parts'=2,'section'=2,'tp'=8] {'tp'}, use_global_device_ids=true, to_apply=%region_3.4.clone | all-reduce | flops 262144 | bytes 1572864
  149.0 0.7 dynamic-slice_convert_fusion
  149.7 0.6 copy.45
  (22 shorter events, 0.8 us)
Async XLA Ops:
  0.6 57.6 %copy-start.1 = (u32[32]{0:T(128)S(1)}, u32[32]{0:T(128)}, u32[]{:S(2)}) copy-start(u32[32]{0:T(128)} %constant.96) | copy-start | bytes 388
  0.6 57.5 %copy-start = (s32[64]{0:T(128)S(1)}, s32[64]{0:T(128)}, u32[]{:S(2)}) copy-start(s32[64]{0:T(128)} %param.10) | copy-start | bytes 772
  48.5 11.0 %collective-permute-start = (bf16[32,256]{1,0:T(8,128)(2,1)S(1)}, bf16[32,256]{1,0:T(8,128)(2,1)S(1)}, u32[]{:S(2)}, u32[]{:S(2)}) collective-permute-start(bf16[32,256]{1,0:T(8,128)(2,1)S(1)} %pad_maximum_fusion), channel_id=1, source_target_pairs={{0,8},{8,0},{1,9},{9,1},{2,10},{10,2},{3,11},{11,3},{4,12},{12,4},... | collective-permute-start | bytes 49160 | tf_op jit(solution)/shard_map/ppermute | solution.py:15
  60.9 88.8 %all-to-all-start = ((bf16[16,8,128]{2,1,0:T(8,128)(2,1)}), bf16[16,8,128]{2,1,0:T(8,128)(2,1)S(1)}, u32[]{:S(2)}, u32[]{:S(2)}) async-start(bf16[16,8,128]{2,1,0:T(8,128)(2,1)} %bitcast.20), calls=%async_computation | async-start | bytes 65536 | tf_op jit(solution)/shard_map/all_to_all | solution.py:107
where the time goes:
time: 151 us; the launch traced here: 150 us
  blocking collectives  106 us (70%)
  matrix products  21.1 us (14%)
  other arithmetic  10.9 us (7%)
  starting transfers between devices  5.83 us (4%)
  local copies, waits for them, and re-layouts  4.85 us (3%)
    unnamed x1, blocking collectives  72.9 us
    all_gather x1, blocking collectives, body(): piece = lax.all_gather(prompt_rows, 'tp', axis=0, tiled=True)  33.3 us
    dot_general x1, matrix products, body(): jnp.dot(attention, output_weight, preferred_element_type=jnp.float32)  8.75 us
    dot_general x1, matrix products, body(): jnp.dot(piece, query_weight, preferred_element_type=jnp.float32)  8.75 us
    all_to_all x1, starting transfers between devices, body(): lax.all_to_all(outgoing, ('section', 'tp'), split_axis=0, concat_axis=2,...  5.82 us
    gather x2, other arithmetic, body(): row_of = page_table[pages] * PAGE + offsets % PAGE  4.6 us
    mul x1, other arithmetic, body(): row_of = page_table[pages] * PAGE + offsets % PAGE  3.23 us
  transfers between devices with their start and end apart: 2, of which 0 were waited for; matrix products, arithmetic and copies ran while one was open for 14% of the time, Pallas kernels for 0%

commit v1 on v0

--- a/solution.py
+++ b/solution.py
@@ -65,7 +65,15 @@
     own_start = section * half_rows
     own_cos = lax.dynamic_slice_in_dim(cosines, own_start, half_rows, 0)
     own_sin = lax.dynamic_slice_in_dim(sines, own_start, half_rows, 0)
-    piece = lax.all_gather(prompt_rows, "tp", axis=0, tiled=True)
+    ways, here = (lax.axis_size("tp"), lax.axis_index("tp"))
+    grown, reach = (prompt_rows, 1)
+    while reach < ways:
+        theirs = lax.ppermute(grown, "tp", [(d, d ^ reach) for d in range(ways)])
+        mine_first = jnp.concatenate([grown, theirs], axis=0)
+        theirs_first = jnp.concatenate([theirs, grown], axis=0)
+        grown = jnp.where(here & reach == 0, mine_first, theirs_first)
+        reach = 2 * reach
+    piece = grown
     query_rows = jnp.dot(piece, query_weight, preferred_element_type=jnp.float32)
     cache_rows = jnp.dot(piece, head_weight, preferred_element_type=jnp.float32)
     joined = jnp.concatenate([query_rows, cache_rows], axis=1)

time: 151 us -> 138 us (0.914)
  blocking collectives: 106 us -> 72.9 us
  waiting for transfers between devices: 0.01 us -> 12 us
  starting transfers between devices: 5.83 us -> 12.3 us
  other arithmetic: 10.9 us -> 12.7 us
    all_gather x1 -> x0, blocking collectives: 33.3 us -> none  [body(): piece = lax.all_gather(prompt_rows, 'tp', axis=0, tiled=True)]
    ppermute x0 -> x3, waiting for transfers between devices: none -> 12 us  [body(): theirs = lax.ppermute(grown, 'tp', [(d, d ^ reach) for d in range(ways)])]
    ppermute x0 -> x3, starting transfers between devices: none -> 7.33 us  [body(): theirs = lax.ppermute(grown, 'tp', [(d, d ^ reach) for d in range(ways)])]
  transfers between devices with their start and end apart: 2 -> 5, of which waited for: 0 -> 2; matrix products, arithmetic and copies ran while one was open for 14% -> 24% of each run, Pallas kernels for 0% -> 0%
where the time goes in v1:
time: 138 us
  blocking collectives  72.9 us (53%)
  matrix products  21.1 us (15%)
  other arithmetic  12.7 us (9%)
  starting transfers between devices  12.3 us (9%)
  waiting for transfers between devices  12 us (9%)
  local copies, waits for them, and re-layouts  5.36 us (4%)
  between operations  1.42 us (1%)
    unnamed x1, blocking collectives  72.9 us
    ppermute x3, waiting for transfers between devices, body(): theirs = lax.ppermute(grown, 'tp', [(d, d ^ reach) for d in range(ways)])  12 us
    dot_general x1, matrix products, body(): jnp.dot(attention, output_weight, preferred_element_type=jnp.float32)  8.75 us
    dot_general x1, matrix products, body(): jnp.dot(piece, query_weight, preferred_element_type=jnp.float32)  8.75 us
    ppermute x3, starting transfers between devices, body(): theirs = lax.ppermute(grown, 'tp', [(d, d ^ reach) for d in range(ways)])  7.33 us
    all_to_all x1, starting transfers between devices, body(): lax.all_to_all(outgoing, ('section', 'tp'), split_axis=0, concat_axis=2,...  4.97 us
    gather x2, other arithmetic, body(): row_of = page_table[pages] * PAGE + offsets % PAGE  4.6 us
    mul x1, other arithmetic, body(): row_of = page_table[pages] * PAGE + offsets % PAGE  3.23 us
  transfers between devices with their start and end apart: 5, of which 2 were waited for; matrix products, arithmetic and copies ran while one was open for 24% of the time, Pallas kernels for 0%

profile of v1, /device:TPU:0, one launch (start us, length us, event | category | flops | bytes accessed | tf_op | source)
XLA Modules:
  0.0 137.7 jit_solution(6664151013857171222)
XLA Ops:
  0.6 3.0 %collective-permute-start = (bf16[4,8192]{1,0:T(4,128)(2,1)}, bf16[4,8192]{1,0:T(4,128)(2,1)S(1)}, u32[]{:S(2)}, u32[]{:S(2)}) collective-permute-start(bf16[4,8192]{1,0:T(4,128)(2,1)} %param.6), channel_id=1, source_target_pairs={{0,1},{1,0},{2,3},{3,2},{4,5},{5,4},{6,7},{7,6},{8,9},{9,8},{10,11... | collective-permute-start | bytes 196616 | tf_op jit(solution)/shard_map/ppermute | solution.py:71
  3.7 1.8 %fusion.46 = (s32[1]{0:T(128)}, s32[1]{0:T(128)}, s32[1]{0:T(128)}, s32[1]{0:T(128)}, s32[1]{0:T(128)}, /*index=5*/s32[1]{0:T(128)}, s32[1]{0:T(128)}, s32[1]{0:...) fusion(s32[12]{0:T(128)} %param.11), kind=kLoop, calls=%fused_computation.79 | loop fusion | bytes 96 | tf_op jit(solution)/shard_map/gather | solution.py:112
  5.4 0.8 compare_bitcast_fusion
  6.7 0.2 compare_reduce_fusion.4
  6.9 4.4 %select_reduce_fusion = s32[64]{0:T(128)S(1)} fusion(s32[]{:T(128)} %bitcast.11, s32[]{:T(128)} %bitcast.12, s32[]{:T(128)} %bitcast.13, s32[]{:T(128)} %bitcast.14, s32[]{:T(128)} %bitcast.15, s32[]{:T(128)} %bitcast.17, s32[]{:T(128)} %bitcast.16, s32[64,1]{1,0:T(8,128)S(1)} %reduce-window.9), kind=kLoop, calls=%fused_computation.38 | loop fusion | flops 1024 | bytes 540 | tf_op jit(solution)/shard_map/gather | solution.py:112
  11.3 3.2 %fusion.31 = s32[64,1]{0,1:T(1,128)S(1)} fusion(pred[64]{0:T(512)(128)(4,1)S(1)} %get-tuple-element.8, pred[64]{0:T(512)(128)(4,1)S(1)} %get-tuple-element.5, pred[64]{0:T(512)(128)(4,1)S(1)} %get-tuple-element.6, pred[64]{0:T(512)(128)(4,1)S(1)} %get-tuple-element.7, pred[64]{0:T(512)(128)(4,1)S(1)} %get-tuple-element.4, s32[64]{0:T(128)S(1)} %select_reduce_fusion, ...), kind=kLoop, calls=%fused_computation.66 | loop fusion | flops 384 | bytes 852 | tf_op jit(solution)/shard_map/mul | solution.py:112
  14.6 0.7 dynamic_slice.14
  15.3 0.7 fusion.26
  16.2 1.0 maximum_select_fusion.2
  17.3 1.6 %collective-permute-start.1 = (bf16[8,8192]{1,0:T(8,128)(2,1)S(1)}, bf16[8,8192]{1,0:T(8,128)(2,1)S(1)}, u32[]{:S(2)}, u32[]{:S(2)}) collective-permute-start(bf16[8,8192]{1,0:T(8,128)(2,1)S(1)} %maximum_select_fusion.2), channel_id=1, source_target_pairs={{0,2},{1,3},{2,0},{3,1},{4,6},{5,7},{6,4},{7,5},{8,10},{9,11},{10,... | collective-permute-start | bytes 393224 | tf_op jit(solution)/shard_map/ppermute | solution.py:71
  18.9 3.4 %collective-permute-done.1 = bf16[8,8192]{1,0:T(8,128)(2,1)S(1)} collective-permute-done((bf16[8,8192]{1,0:T(8,128)(2,1)S(1)}, bf16[8,8192]{1,0:T(8,128)(2,1)S(1)}, u32[]{:S(2)}, u32[]{:S(2)}) %collective-permute-start.1) | collective-permute-done | bytes 131104 | tf_op jit(solution)/shard_map/ppermute | solution.py:71
  22.3 2.7 %collective-permute-start.2 = (bf16[16,8192]{1,0:T(8,128)(2,1)S(1)}, bf16[16,8192]{1,0:T(8,128)(2,1)S(1)}, u32[]{:S(2)}, u32[]{:S(2)}) collective-permute-start(bf16[16,8192]{1,0:T(8,128)(2,1)S(1)} %maximum_select_fusion.1), channel_id=1, source_target_pairs={{0,4},{1,5},{2,6},{3,7},{4,0},{5,1},{6,2},{7,3},{8,12},{9,13},{10,... | collective-permute-start | bytes 786440 | tf_op jit(solution)/shard_map/ppermute | solution.py:71
  25.0 1.2 dynamic-slice
  27.0 8.6 %collective-permute-done.2 = bf16[16,8192]{1,0:T(8,128)(2,1)S(1)} collective-permute-done((bf16[16,8192]{1,0:T(8,128)(2,1)S(1)}, bf16[16,8192]{1,0:T(8,128)(2,1)S(1)}, u32[]{:S(2)}, u32[]{:S(2)}) %collective-permute-start.2) | collective-permute-done | bytes 262176 | tf_op jit(solution)/shard_map/ppermute | solution.py:71
  35.5 3.0 %fusion.1 = f32[32,256]{1,0:T(8,128)S(1)} fusion(bf16[1,8192,256]{2,1,0:T(8,128)(2,1)} %param.8, bf16[16,8192]{1,0:T(8,128)(2,1)S(1)} %collective-permute-done.2, bf16[16,8192]{1,0:T(8,128)(2,1)S(1)} %maximum_select_fusion.1, pred[]{:T(512)S(6)} %eq.46), kind=kOutput, calls=%fused_computation.2 | convolution fusion | flops 136577024 | bytes 4751361 | tf_op jit(solution)/shard_map/dot_general | solution.py:78
  38.8 8.7 %convolution_bitcast_fusion = f32[4,8,8,128]{3,1,2,0:T(8,128)S(1)} fusion(bf16[8192,1024]{1,0:T(8,128)(2,1)} %param.7, bf16[16,8192]{1,0:T(8,128)(2,1)S(1)} %collective-permute-done.2, bf16[16,8192]{1,0:T(8,128)(2,1)S(1)} %maximum_select_fusion.1, pred[]{:T(512)S(6)} %eq.46), kind=kOutput, calls=%fused_computation.6 | convolution fusion | flops 539230208 | bytes 17432576 | tf_op jit(solution)/shard_map/dot_general | solution.py:77
  47.9 1.3 scatter_custom_fusion
  49.2 5.0 %all-to-all-start = ((bf16[16,8,128]{2,1,0:T(8,128)(2,1)}), bf16[16,8,128]{2,1,0:T(8,128)(2,1)S(1)}, u32[]{:S(2)}, u32[]{:S(2)}) async-start(bf16[16,8,128]{2,1,0:T(8,128)(2,1)} %bitcast.19), calls=%async_computation | async-start | bytes 65536 | tf_op jit(solution)/shard_map/all_to_all | solution.py:115
  54.2 0.4 fusion.47
  54.6 0.2 fusion.7
  54.8 8.7 %fusion.8 = f32[32,8192]{1,0:T(8,128)S(1)} fusion(bf16[1024,8192]{1,0:T(8,128)(2,1)} %param.9, bf16[8,4,8,128]{3,2,1,0:T(8,128)(2,1)S(1)} %fusion.7), kind=kOutput, calls=%fused_computation.21 | convolution fusion | flops 536870912 | bytes 17891328 | tf_op jit(solution)/shard_map/dot_general | solution.py:103
  63.5 72.9 %all-reduce.2 = bf16[32,8192]{1,0:T(8,128)(2,1)S(1)} all-reduce(f32[32,8192]{1,0:T(8,128)S(1)} %fusion.8), channel_id=2, replica_groups=mesh['parts'=2,'section'=2,'tp'=8] {'tp'}, use_global_device_ids=true, to_apply=%region_3.4.clone | all-reduce | flops 262144 | bytes 1572864
  136.4 0.7 dynamic-slice_convert_fusion
  137.1 0.6 copy.48
  (24 shorter events, 1.3 us)
Async XLA Ops:
  0.6 15.6 %collective-permute-start = (bf16[4,8192]{1,0:T(4,128)(2,1)}, bf16[4,8192]{1,0:T(4,128)(2,1)S(1)}, u32[]{:S(2)}, u32[]{:S(2)}) collective-permute-start(bf16[4,8192]{1,0:T(4,128)(2,1)} %param.6), channel_id=1, source_target_pairs={{0,1},{1,0},{2,3},{3,2},{4,5},{5,4},{6,7},{7,6},{8,9},{9,8},{10,11... | collective-permute-start | bytes 196616 | tf_op jit(solution)/shard_map/ppermute | solution.py:71
  17.3 5.0 %collective-permute-start.1 = (bf16[8,8192]{1,0:T(8,128)(2,1)S(1)}, bf16[8,8192]{1,0:T(8,128)(2,1)S(1)}, u32[]{:S(2)}, u32[]{:S(2)}) collective-permute-start(bf16[8,8192]{1,0:T(8,128)(2,1)S(1)} %maximum_select_fusion.2), channel_id=1, source_target_pairs={{0,2},{1,3},{2,0},{3,1},{4,6},{5,7},{6,4},{7,5},{8,10},{9,11},{10,... | collective-permute-start | bytes 393224 | tf_op jit(solution)/shard_map/ppermute | solution.py:71
  22.3 13.2 %collective-permute-start.2 = (bf16[16,8192]{1,0:T(8,128)(2,1)S(1)}, bf16[16,8192]{1,0:T(8,128)(2,1)S(1)}, u32[]{:S(2)}, u32[]{:S(2)}) collective-permute-start(bf16[16,8192]{1,0:T(8,128)(2,1)S(1)} %maximum_select_fusion.1), channel_id=1, source_target_pairs={{0,4},{1,5},{2,6},{3,7},{4,0},{5,1},{6,2},{7,3},{8,12},{9,13},{10,... | collective-permute-start | bytes 786440 | tf_op jit(solution)/shard_map/ppermute | solution.py:71
  38.8 9.0 %collective-permute-start.3 = (bf16[32,256]{1,0:T(8,128)(2,1)S(1)}, bf16[32,256]{1,0:T(8,128)(2,1)S(1)}, u32[]{:S(2)}, u32[]{:S(2)}) collective-permute-start(bf16[32,256]{1,0:T(8,128)(2,1)S(1)} %pad_maximum_fusion), channel_id=1, source_target_pairs={{0,8},{8,0},{1,9},{9,1},{2,10},{10,2},{3,11},{11,3},{4,12},{12,4},... | collective-permute-start | bytes 49160 | tf_op jit(solution)/shard_map/ppermute | solution.py:15
  49.2 87.9 %all-to-all-start = ((bf16[16,8,128]{2,1,0:T(8,128)(2,1)}), bf16[16,8,128]{2,1,0:T(8,128)(2,1)S(1)}, u32[]{:S(2)}, u32[]{:S(2)}) async-start(bf16[16,8,128]{2,1,0:T(8,128)(2,1)} %bitcast.19), calls=%async_computation | async-start | bytes 65536 | tf_op jit(solution)/shard_map/all_to_all | solution.py:115
